TPU v7x, 32 devices: a whole 2x2x4 slice. The times are simulated.
32 devices in a mesh: group: 4 (over z), dom: 8 (over y, x, core).
Axes of the slice: x: 2, y: 2, z: 4, core: 2. Of those that a mesh axis runs over, the one named last changes fastest.
Arguments:
- features: bfloat16 [16384, 128], P(('group', 'dom')), may hold values from -6 to 6
- cotangent: bfloat16 [16384, 128], P(('group', 'dom')), may hold values from -6 to 6
- fine_send: int32 [256, 16], P(('group', 'dom')), may hold values from 0 to 512, as said below
- fine_rim: int32 [64, 128], P(('group', 'dom')), may hold values from 0 to 511
- fine_src: int32 [131072], P(('group', 'dom')), may hold values from 0 to 895, as said below
- fine_dst: int32 [131072], P(('group', 'dom')), may hold values from 0 to 511
- fine_pool: int32 [16384], P(('group', 'dom')), may hold values from 0 to 255, as said below
- coarse_send: int32 [256, 4], P(('group', 'dom')), may hold values from 0 to 32, as said below
- coarse_src: int32 [8192], P(('group', 'dom')), may hold values from 0 to 63, as said below
- coarse_dst: int32 [8192], P(('group', 'dom')), may hold values from 0 to 31
- coarse_pool: int32 [1024], P(('group', 'dom')), may hold values from 0 to 511
- w_send: bfloat16 [128, 128], replicated, may hold values from -0.5 to 0.5
- w_recv: bfloat16 [128, 128], replicated, may hold values from -0.5 to 0.5
- w_node: bfloat16 [128, 128], replicated, may hold values from -0.5 to 0.5
- v_send: bfloat16 [128, 128], replicated, may hold values from -0.5 to 0.5
- v_recv: bfloat16 [128, 128], replicated, may hold values from -0.5 to 0.5
- v_node: bfloat16 [128, 128], replicated, may hold values from -0.5 to 0.5
- w_top: bfloat16 [128, 128], replicated, may hold values from -0.5 to 0.5
Outputs:
- flow: bfloat16 [16384, 128], P(('group', 'dom'))
- grad_features: float32 [16384, 128], P(('group', 'dom'))
- grad_send: float32 [128, 128], replicated
Inputs may be any that keep to these rules, and one draw needn't show every extreme that they name: `fine_send`: each device holds 8 rows of 16: row p lists own node rows for the device with dom index p of its group; the value 512 marks an empty slot, live slots come first, and three rows of every device are full. `fine_rim`: each device holds two rows: the first go to the previous group's device of the same dom index, the second to the next group's. `fine_src`: index into the device's extended rows: its 512 nodes, 128 rows from its group in dom order, 128 rows from the previous group, 128 from the next. `fine_pool`: coarse node numbered within the node's group. `coarse_send`: as fine_send with 4 slots a row and 32 marking an empty slot. `coarse_src`: index into the device's coarse rows, then 8 * 4 rows from its group in dom order.
All inputs are finite; a program needn't handle non-finite values.
Results may differ from a plain program's by a relative error of at most 0.025.
Values may be sent and summed in bfloat16 or wider, within the bound.
No kernel may reach another device: no remote copies, remote signals or barrier semaphores. Data moves between devices by JAX's collectives and lax.ppermute only.
A program may use at most 64 MiB of HBM per device.

v0:
```python
import jax
import jax.numpy as jnp
from jax import lax
from jax.sharding import PartitionSpec as P

NCC = 512


def with_halo(block, sides, width):
    for axis, dim in sides:
        count = lax.axis_size(axis)
        forward = [(i, i + 1) for i in range(count - 1)]
        backward = [(target, source) for source, target in forward]
        low = lax.ppermute(
            lax.slice_in_dim(block, block.shape[dim] - width, None, axis=dim), axis, forward
        )
        high = lax.ppermute(lax.slice_in_dim(block, 0, width, axis=dim), axis, backward)
        block = jnp.concatenate([low, block, high], axis=dim)
    return block


def silu_slope(values):
    sigma = jax.nn.sigmoid(values)
    return sigma * (1.0 + values * (1.0 - sigma))


def edge_forward(extended, own_rows, sources, targets, w_send, w_recv, w_node):
    preact = jnp.dot(extended[sources], w_send, preferred_element_type=jnp.float32)
    preact = preact + jnp.dot(own_rows[targets], w_recv, preferred_element_type=jnp.float32)
    message = jax.nn.silu(preact).astype(jnp.bfloat16)
    summed = jax.ops.segment_sum(
        message.astype(jnp.float32), targets, num_segments=own_rows.shape[0]
    ).astype(jnp.bfloat16)
    updated = (
        own_rows.astype(jnp.float32) + jnp.dot(summed, w_node, preferred_element_type=jnp.float32)
    ).astype(jnp.bfloat16)
    return (updated, preact)


def edge_backward(grad_out, extended, own_rows, preact, sources, targets, w_send, w_recv, w_node):
    rounded = grad_out.astype(jnp.bfloat16)
    grad_sum = jnp.dot(rounded, w_node.T, preferred_element_type=jnp.float32)
    grad_pre = (grad_sum[targets] * silu_slope(preact)).astype(jnp.bfloat16)
    grad_ext = jax.ops.segment_sum(
        jnp.dot(grad_pre, w_send.T, preferred_element_type=jnp.float32),
        sources,
        num_segments=extended.shape[0],
    )
    own_count = own_rows.shape[0]
    grad_own = grad_out + jax.ops.segment_sum(
        jnp.dot(grad_pre, w_recv.T, preferred_element_type=jnp.float32),
        targets,
        num_segments=own_count,
    )
    grad_own = grad_own + grad_ext[:own_count]
    grad_weight = lax.dot_general(
        extended[sources], grad_pre, (((0,), (0,)), ((), ())), preferred_element_type=jnp.float32
    )
    return (grad_own, grad_ext[own_count:], grad_weight)


def top_forward(pooled, w_top):
    slope_in = jnp.dot(pooled.astype(jnp.bfloat16), w_top, preferred_element_type=jnp.float32)
    return ((pooled + jax.nn.silu(slope_in)).astype(jnp.bfloat16), slope_in)


def top_backward(grad_top, slope_in, w_top):
    inner = (grad_top * silu_slope(slope_in)).astype(jnp.bfloat16)
    return grad_top + jnp.dot(inner, w_top.T, preferred_element_type=jnp.float32)


def add_rows(grads, index, values):
    padded = jnp.concatenate([grads, jnp.zeros((1, grads.shape[1]), jnp.float32)], axis=0)
    return padded.at[index].add(values)[:-1]


def local(
    features,
    cotangent,
    fine_send,
    fine_rim,
    fine_src,
    fine_dst,
    fine_pool,
    coarse_send,
    coarse_src,
    coarse_dst,
    coarse_pool,
    w_send,
    w_recv,
    w_node,
    v_send,
    v_recv,
    v_node,
    w_top,
):
    width = features.shape[1]
    dom_count = lax.axis_size("dom")
    coarse_count = coarse_pool.shape[0]
    group_coarse = coarse_count * dom_count
    slot_rows = fine_send.shape[1]
    coarse_slots = coarse_send.shape[1]
    rim_count = fine_rim.shape[1]
    padded = jnp.concatenate([features, jnp.zeros((1, width), jnp.bfloat16)], axis=0)
    incoming = lax.all_to_all(
        padded[fine_send], "dom", split_axis=0, concat_axis=0, tiled=True
    ).reshape(-1, width)
    rim_rows = with_halo(features[fine_rim], (("group", 0),), 1)
    extended = jnp.concatenate([features, incoming, rim_rows[0], rim_rows[3]], axis=0)
    updated, preact = edge_forward(extended, features, fine_src, fine_dst, w_send, w_recv, w_node)
    partial_value = jax.ops.segment_sum(
        updated.astype(jnp.float32), fine_pool, num_segments=group_coarse
    )
    grad_flow = cotangent.astype(jnp.float32)
    grad_partial = jax.ops.segment_sum(grad_flow, fine_pool, num_segments=group_coarse)
    owned = lax.psum_scatter(partial_value, "dom", scatter_dimension=0, tiled=True)
    grad_coarse = lax.psum_scatter(grad_partial, "dom", scatter_dimension=0, tiled=True)
    coarse_in = (0.25 * owned).astype(jnp.bfloat16)
    cpadded = jnp.concatenate([coarse_in, jnp.zeros((1, width), jnp.bfloat16)], axis=0)
    cincoming = lax.all_to_all(
        cpadded[coarse_send], "dom", split_axis=0, concat_axis=0, tiled=True
    ).reshape(-1, width)
    cextended = jnp.concatenate([coarse_in, cincoming], axis=0)
    coarse_mid, cpreact = edge_forward(
        cextended, coarse_in, coarse_src, coarse_dst, v_send, v_recv, v_node
    )
    top_partial = jax.ops.segment_sum(coarse_mid.astype(jnp.float32), coarse_pool, num_segments=NCC)
    grad_top_partial = jax.ops.segment_sum(grad_coarse, coarse_pool, num_segments=NCC)
    top_total = lax.psum(top_partial, ("group", "dom"))
    grad_top = lax.psum(grad_top_partial, ("group", "dom"))
    pooled = 0.125 * top_total
    top_out, slope_in = top_forward(pooled, w_top)
    coarse_out = (coarse_mid.astype(jnp.float32) + top_out[coarse_pool].astype(jnp.float32)).astype(
        jnp.bfloat16
    )
    coarse_table = lax.all_gather(coarse_out, "dom", axis=0, tiled=True)
    flow = (updated.astype(jnp.float32) + coarse_table[fine_pool].astype(jnp.float32)).astype(
        jnp.bfloat16
    )
    grad_pool = top_backward(grad_top, slope_in, w_top)
    grad_cmid = grad_coarse + 0.125 * grad_pool[coarse_pool]
    c_own, c_halo, c_weight = edge_backward(
        grad_cmid, cextended, coarse_in, cpreact, coarse_src, coarse_dst, v_send, v_recv, v_node
    )
    creturned = lax.all_to_all(
        c_halo.reshape(dom_count, coarse_slots, width),
        "dom",
        split_axis=0,
        concat_axis=0,
        tiled=True,
    )
    grad_cin = add_rows(c_own, coarse_send.reshape(-1), creturned.reshape(-1, width))
    grad_table = lax.all_gather(grad_cin, "dom", axis=0, tiled=True)
    grad_fmid = grad_flow + 0.25 * grad_table[fine_pool]
    f_own, f_halo, f_weight = edge_backward(
        grad_fmid, extended, features, preact, fine_src, fine_dst, w_send, w_recv, w_node
    )
    split = dom_count * slot_rows
    returned = lax.all_to_all(
        f_halo[:split].reshape(dom_count, slot_rows, width),
        "dom",
        split_axis=0,
        concat_axis=0,
        tiled=True,
    )
    grad_x = add_rows(f_own, fine_send.reshape(-1), returned.reshape(-1, width))
    rim_grads = jnp.stack([f_halo[split : split + rim_count], f_halo[split + rim_count :]], axis=0)
    rim_back = with_halo(rim_grads, (("group", 0),), 1)
    rim_values = jnp.concatenate([rim_back[0], rim_back[3]], axis=0)
    grad_x = add_rows(grad_x, fine_rim.reshape(-1), rim_values)
    grad_send = lax.psum(f_weight, ("group", "dom"))
    return (flow, grad_x, grad_send)


def solution(mesh):
    placed = (
        P(("group", "dom"), None),
        P(("group", "dom"), None),
        P(("group", "dom"), None),
        P(("group", "dom"), None),
        P(("group", "dom")),
        P(("group", "dom")),
        P(("group", "dom")),
        P(("group", "dom"), None),
        P(("group", "dom")),
        P(("group", "dom")),
        P(("group", "dom")),
        P(),
        P(),
        P(),
        P(),
        P(),
        P(),
        P(),
    )
    return jax.shard_map(
        local,
        mesh=mesh,
        in_specs=placed,
        out_specs=(P(("group", "dom"), None), P(("group", "dom"), None), P()),
        check_vma=False,
    )
```

profile of v0, /device:TPU:1, one launch (start us, length us, event | category | flops | bytes accessed | tf_op | source)
XLA Modules:
  0.0 539.3 jit_solution(17636104793602975725)
XLA Ops:
  10.9 4.6 collective-permute-start
  18.6 5.1 all-to-all-start
  24.4 12.1 %gather_fusion.3 = bf16[4096,128]{1,0:T(8,128)(2,1)S(1)} fusion(bf16[512,128]{1,0:T(8,128)(2,1)S(1)} %copy-done.1, s32[4096]{0:T(1024)S(1)} %fusion.37), kind=kCustom, calls=%fused_computation.3 | custom fusion | bytes 2113536 | tf_op jit(solution)/shard_map/gather | solution.py:29
  38.4 12.1 %gather_fusion.2 = bf16[4096,128]{1,0:T(8,128)(2,1)S(1)} fusion(bf16[896,128]{1,0:T(8,128)(2,1)S(1)} %pad_maximum_fusion, s32[4096]{0:T(1024)S(1)} %fusion.36), kind=kCustom, calls=%fused_computation.2 | custom fusion | bytes 2113536 | tf_op jit(solution)/shard_map/gather | solution.py:28
  50.5 2.0 convolution_add_fusion
  52.6 23.8 %scatter_custom_fusion = f32[512,128]{1,0:T(8,128)} fusion(s32[4096]{0:T(1024)} %param.23, f32[4096,128]{1,0:T(8,128)S(1)} %convolution_add_fusion, f32[]{:T(128)} %constant.20.clone.1, f32[]{:T(128)} %constant.14.clone.1), kind=kCustom, calls=%fused_computation.28 | custom fusion | flops 3670016 | bytes 2360320 | tf_op jit(solution)/shard_map/scatter-add | solution.py:31
  78.2 3.2 scatter_custom_fusion.1
  81.5 3.0 scatter_custom_fusion.4
  91.4 23.3 %reduce-scatter.3.cloned.1.call-done = f32[32,128]{1,0:T(8,128)} async-done(((f32[256,128]{1,0:T(8,128)}), f32[32,128]{1,0:T(8,128)}) %reduce-scatter.3.cloned.1.call-update) | async-done | bytes 16400 | tf_op jit(solution)/shard_map/reduce_scatter | solution.py:116
  116.6 4.5 all-to-all-start.1
  121.6 30.2 %reduce-scatter.5.cloned.1.call-done = f32[32,128]{1,0:T(8,128)} async-done(((f32[256,128]{1,0:T(8,128)}), f32[32,128]{1,0:T(8,128)}) %reduce-scatter.5.cloned.1.call-update) | async-done | bytes 16400 | tf_op jit(solution)/shard_map/reduce_scatter | solution.py:117
  162.0 126.7 %all-reduce.10.cloned.1.call-done = (f32[512,128]{1,0:T(8,128)}, f32[512,128]{1,0:T(8,128)}) async-done(((f32[512,128]{1,0:T(8,128)}, f32[512,128]{1,0:T(8,128)}), (f32[512,128]{1,0:T(8,128)}, f32[512,128]{1,0:T(8,128)})) %all-reduce.10.cloned.1.call-update) | async-done | bytes 524304 | tf_op jit(solution)/shard_map/psum | solution.py:129
  291.4 10.7 %all_gather.6 = bf16[256,128]{1,0:T(8,128)(2,1)S(1)} all-gather(bf16[32,128]{1,0:T(8,128)(2,1)S(1)} %add_convert_fusion.2), channel_id=1, replica_groups=mesh['group'=4,'dom'=8] {'dom'}, dimensions={0}, use_global_device_ids=true | all-gather | bytes 73728 | tf_op jit(solution)/shard_map/all_gather | solution.py:136
  305.2 2.1 convolution_add_fusion.1
  314.8 3.4 all-to-all-start.2
  323.0 8.8 %all_gather.7 = f32[256,128]{1,0:T(8,128)S(1)} all-gather(f32[32,128]{1,0:T(8,128)S(1)} %slice.78), channel_id=1, replica_groups=mesh['group'=4,'dom'=8] {'dom'}, dimensions={0}, use_global_device_ids=true | all-gather | bytes 147456 | tf_op jit(solution)/shard_map/all_gather | solution.py:153
  334.7 14.2 %gather_fusion.12 = f32[4096,128]{1,0:T(8,128)} fusion(f32[512,128]{1,0:T(8,128)S(1)} %fusion.15, s32[4096]{0:T(1024)S(1)} %fusion.37), kind=kCustom, calls=%fused_computation.12 | custom fusion | bytes 4210688 | tf_op jit(solution)/shard_map/gather | solution.py:43
  348.9 2.4 multiply_convert_fusion
  354.6 22.8 %scatter_custom_fusion.9 = f32[896,128]{1,0:T(8,128)S(1)} fusion(s32[4096]{0:T(1024)} %param.22, f32[4096,128]{1,0:T(8,128)} %fusion.56, f32[]{:T(128)} %constant.14.clone.1), kind=kCustom, calls=%fused_computation.54 | custom fusion | flops 524288 | bytes 459264 | tf_op jit(solution)/shard_map/scatter-add | solution.py:44
  378.0 3.4 all-to-all-start.3
  382.5 22.5 %scatter_fusion.2 = f32[512,128]{1,0:T(8,128)S(1)} fusion(f32[512,128]{1,0:T(8,128)S(1)} %slice_add_fusion, s32[4096]{0:T(1024)S(1)} %copy-done.10, f32[4096,128]{1,0:T(8,128)S(1)} %fusion.57), kind=kCustom, calls=%fused_computation.23 | custom fusion | flops 524288 | bytes 6307840 | tf_op jit(solution)/shard_map/scatter-add | solution.py:50
  406.3 4.0 collective-permute-start.2
  411.8 2.1 scatter_custom_fusion.12
  414.7 116.5 %all-reduce.8.cloned.1.call-done = f32[128,128]{1,0:T(8,128)} async-done(((f32[128,128]{1,0:T(8,128)}), f32[128,128]{1,0:T(8,128)}) %all-reduce.8.cloned.1.call-update) | async-done | bytes 65552 | tf_op jit(solution)/shard_map/psum | solution.py:171
  (133 shorter events, 61.4 us)
Async XLA Ops:
  7.2 43.4 %copy-start = (bf16[128,128]{1,0:T(8,128)(2,1)S(1)}, bf16[128,128]{1,0:T(8,128)(2,1)}, u32[]{:S(2)}) copy-start(bf16[128,128]{1,0:T(8,128)(2,1)} %param.29) | copy-start | bytes 98308
  9.6 28.8 %collective-permute-start.1 = (bf16[1,128,128]{2,1,0:T(8,128)(2,1)S(1)}, bf16[1,128,128]{2,1,0:T(8,128)(2,1)S(1)}, u32[]{:S(2)}, u32[]{:S(2)}) collective-permute-start(bf16[1,128,128]{2,1,0:T(8,128)(2,1)S(1)} %get-tuple-element.9), channel_id=1, source_target_pairs={{8,0},{16,8},{24,16},{9,1},{17,9},{25,17},{10,2},{18,10},{26,18},{... | collective-permute-start | bytes 98312 | tf_op jit(solution)/shard_map/ppermute | solution.py:17
  10.9 27.5 %collective-permute-start = (bf16[1,128,128]{2,1,0:T(8,128)(2,1)S(1)}, bf16[1,128,128]{2,1,0:T(8,128)(2,1)S(1)}, u32[]{:S(2)}, u32[]{:S(2)}) collective-permute-start(bf16[1,128,128]{2,1,0:T(8,128)(2,1)S(1)} %get-tuple-element.8), channel_id=1, source_target_pairs={{0,8},{8,16},{16,24},{1,9},{9,17},{17,25},{2,10},{10,18},{18,26},{... | collective-permute-start | bytes 98312 | tf_op jit(solution)/shard_map/ppermute | solution.py:14
  18.6 19.8 %all-to-all-start = ((bf16[8,16,128]{2,1,0:T(8,128)(2,1)}), bf16[8,16,128]{2,1,0:T(8,128)(2,1)S(1)}, u32[]{:S(2)}, u32[]{:S(2)}) async-start(bf16[8,16,128]{2,1,0:T(8,128)(2,1)} %bitcast), calls=%async_computation | async-start | bytes 65536 | tf_op jit(solution)/shard_map/all_to_all | solution.py:105
  23.7 91.0 %reduce-scatter.3.cloned.1.call-start = ((), (), s32[]{:S(2)}) async-start(), calls=%async_computation.6 | async-start | bytes 147456 | tf_op jit(solution)/shard_map/reduce_scatter | solution.py:116
  52.6 29.0 %copy-start.3 = (bf16[512,128]{1,0:T(8,128)(2,1)S(1)}, bf16[512,128]{1,0:T(8,128)(2,1)}, u32[]{:S(2)}) copy-start(bf16[512,128]{1,0:T(8,128)(2,1)} %param.19) | copy-start | bytes 393220
  76.4 78.8 %copy-start.5 = (bf16[128,128]{1,0:T(8,128)(2,1)S(1)}, bf16[128,128]{1,0:T(8,128)(2,1)}, u32[]{:S(2)}) copy-start(bf16[128,128]{1,0:T(8,128)(2,1)} %param.32) | copy-start | bytes 98308
  76.4 81.5 %copy-start.7 = (bf16[128,128]{1,0:T(8,128)(2,1)S(1)}, bf16[128,128]{1,0:T(8,128)(2,1)}, u32[]{:S(2)}) copy-start(bf16[128,128]{1,0:T(8,128)(2,1)} %param.34) | copy-start | bytes 98308
  81.5 70.4 %reduce-scatter.5.cloned.1.call-start = ((), (), s32[]{:S(2)}) async-start(), calls=%async_computation.7 | async-start | bytes 147456 | tf_op jit(solution)/shard_map/reduce_scatter | solution.py:117
  89.6 64.7 %copy-start.16 = (s32[1024]{0:T(1024)}, s32[1024]{0:T(1024)S(1)}, u32[]{:S(2)}) copy-start(s32[1024]{0:T(1024)S(1)} %pad_clamp_fusion.2) | copy-start | bytes 12292
  116.6 37.7 %all-to-all-start.1 = ((bf16[8,4,128]{2,1,0:T(4,128)(2,1)}), bf16[8,4,128]{2,1,0:T(4,128)(2,1)S(1)}, u32[]{:S(2)}, u32[]{:S(2)}) async-start(bf16[8,4,128]{2,1,0:T(4,128)(2,1)} %bitcast.7), calls=%async_computation.2 | async-start | bytes 16384 | tf_op jit(solution)/shard_map/all_to_all | solution.py:120
  121.0 167.7 %all-reduce.10.cloned.1.call-start = ((), (), s32[]{:S(2)}) async-start(), calls=%async_computation.9 | async-start | bytes 1048576 | tf_op jit(solution)/shard_map/psum | solution.py:129
  311.5 20.4 %copy-start.15 = (s32[1024]{0:T(1024)S(1)}, s32[1024]{0:T(1024)}, u32[]{:S(2)}) copy-start(s32[1024]{0:T(1024)} %pad_clamp_fusion) | copy-start | bytes 12292
  314.8 7.5 %all-to-all-start.2 = ((f32[8,4,128]{2,1,0:T(4,128)}), f32[8,4,128]{2,1,0:T(4,128)S(1)}, u32[]{:S(2)}, u32[]{:S(2)}) async-start(f32[8,4,128]{2,1,0:T(4,128)} %bitcast.10), calls=%async_computation.4 | async-start | bytes 32768 | tf_op jit(solution)/shard_map/all_to_all | solution.py:145
  353.4 28.0 %copy-start.2 = (f32[512,128]{1,0:T(8,128)S(1)}, f32[512,128]{1,0:T(8,128)}, u32[]{:S(2)}) copy-start(f32[512,128]{1,0:T(8,128)} %gather_fusion.11) | copy-start | bytes 786436
  353.4 29.0 %copy-start.10 = (s32[4096]{0:T(1024)S(1)}, s32[4096]{0:T(1024)}, u32[]{:S(2)}) copy-start(s32[4096]{0:T(1024)} %param.23) | copy-start | bytes 49156
  378.0 32.3 %all-to-all-start.3 = ((f32[8,16,128]{2,1,0:T(8,128)}), f32[8,16,128]{2,1,0:T(8,128)S(1)}, u32[]{:S(2)}, u32[]{:S(2)}) async-start(f32[8,16,128]{2,1,0:T(8,128)} %bitcast.13), calls=%async_computation.5 | async-start | bytes 131072 | tf_op jit(solution)/shard_map/all_to_all | solution.py:159
  381.4 149.8 %all-reduce.8.cloned.1.call-start = ((), (), s32[]{:S(2)}) async-start(), calls=%async_computation.8 | async-start | bytes 131072 | tf_op jit(solution)/shard_map/psum | solution.py:171
  382.4 22.6 %copy-start.13 = (f32[1,128,128]{2,1,0:T(8,128)S(1)}, f32[1,128,128]{2,1,0:T(8,128)}, u32[]{:S(2)}) copy-start(f32[1,128,128]{2,1,0:T(8,128)} %get-tuple-element.6) | copy-start | bytes 196612
  382.4 23.9 %copy-start.12 = (f32[1,128,128]{2,1,0:T(8,128)S(1)}, f32[1,128,128]{2,1,0:T(8,128)}, u32[]{:S(2)}) copy-start(f32[1,128,128]{2,1,0:T(8,128)} %get-tuple-element.5) | copy-start | bytes 196612
  382.4 27.9 %copy-start.19 = (s32[128]{0:T(128)S(1)}, s32[128]{0:T(128)}, u32[]{:S(2)}) copy-start(s32[128]{0:T(128)} %fusion.46) | copy-start | bytes 1540
  382.4 29.2 %copy-start.18 = (pred[513]{0:T(1024)(128)(4,1)S(1)}, pred[513]{0:T(1024)(128)(4,1)}, u32[]{:S(2)}) copy-start(pred[513]{0:T(1024)(128)(4,1)} %constant.27.clone.1) | copy-start | bytes 1543
  405.0 6.8 %collective-permute-start.3 = (f32[1,128,128]{2,1,0:T(8,128)S(1)}, f32[1,128,128]{2,1,0:T(8,128)S(1)}, u32[]{:S(2)}, u32[]{:S(2)}) collective-permute-start(f32[1,128,128]{2,1,0:T(8,128)S(1)} %copy-done.13), channel_id=1, source_target_pairs={{8,0},{16,8},{24,16},{9,1},{17,9},{25,17},{10,2},{18,10},{26,18},{... | collective-permute-start | bytes 196616 | tf_op jit(solution)/shard_map/ppermute | solution.py:17
  406.3 5.5 %collective-permute-start.2 = (f32[1,128,128]{2,1,0:T(8,128)S(1)}, f32[1,128,128]{2,1,0:T(8,128)S(1)}, u32[]{:S(2)}, u32[]{:S(2)}) collective-permute-start(f32[1,128,128]{2,1,0:T(8,128)S(1)} %copy-done.12), channel_id=1, source_target_pairs={{0,8},{8,16},{16,24},{1,9},{9,17},{17,25},{2,10},{10,18},{18,26},{... | collective-permute-start | bytes 196616 | tf_op jit(solution)/shard_map/ppermute | solution.py:14
  (9 other events, 102.8 us)
Sparse Core Ops, SparseCore 0:
  81.6 33.0 reduce-scatter.2
  118.3 33.5 reduce-scatter.4
  159.6 129.0 all-reduce.9
  410.4 120.7 all-reduce.7
where the time goes:
time: 541 us; the launch traced here: 539 us
  waiting for transfers between devices  299 us (55%)
  other arithmetic  105 us (19%)
  local copies, waits for them, and re-layouts  57.2 us (11%)
  starting transfers between devices  27.6 us (5%)
  blocking collectives  19.5 us (4%)
  matrix products  16.5 us (3%)
  between operations  14.3 us (3%)
    psum x1, waiting for transfers between devices, local(): top_total = lax.psum(top_partial, ('group', 'dom'))  127 us
    psum x1, waiting for transfers between devices, local(): grad_send = lax.psum(f_weight, ('group', 'dom'))  117 us
    reduce_scatter x1, waiting for transfers between devices, local(): lax.psum_scatter(grad_partial, 'dom', scatter_dimension=0, tiled=True)  30.2 us
    scatter-add x2, other arithmetic, edge_forward(): jax.ops.segment_sum(message.astype(jnp.float32), targets, num_segments=ow...  25.4 us
    scatter-add x2, other arithmetic, edge_backward(): jax.ops.segment_sum(jnp.dot(grad_pre, w_recv.T, preferred_element_type=jn...  24.4 us
    scatter-add x2, other arithmetic, edge_backward(): jax.ops.segment_sum(jnp.dot(grad_pre, w_send.T, preferred_element_type=jn...  24.3 us
    reduce_scatter x1, waiting for transfers between devices, local(): lax.psum_scatter(partial_value, 'dom', scatter_dimension=0, tiled=True)  23.3 us
    gather x2, local copies, waits for them, and re-layouts, edge_backward(): grad_pre = (grad_sum[targets] * silu_slope(preact)).astype(jnp.bfloat16)  15.8 us
  transfers between devices with their start and end apart: 12, of which 5 were waited for; matrix products, arithmetic and copies ran while one was open for 12% of the time, Pallas kernels for 0%

commit v1 on v0

--- a/solution.py
+++ b/solution.py
@@ -126,7 +126,7 @@
     )
     top_partial = jax.ops.segment_sum(coarse_mid.astype(jnp.float32), coarse_pool, num_segments=NCC)
     grad_top_partial = jax.ops.segment_sum(grad_coarse, coarse_pool, num_segments=NCC)
-    top_total = lax.psum(top_partial, ("group", "dom"))
+    top_total = jnp.sum(lax.all_gather(top_partial, ("group", "dom")), axis=0)
     grad_top = lax.psum(grad_top_partial, ("group", "dom"))
     pooled = 0.125 * top_total
     top_out, slope_in = top_forward(pooled, w_top)

time: 541 us -> 615 us (1.14)
  waiting for transfers between devices: 299 us -> 370 us
    all_gather x0 -> x1, waiting for transfers between devices: none -> 79.9 us  [local(): top_total = jnp.sum(lax.all_gather(top_partial, ('group', 'dom')), axis=0)]
    reduce_scatter x1, waiting for transfers between devices: 30.2 us -> 15.8 us  [local(): lax.psum_scatter(grad_partial, 'dom', scatter_dimension=0, tiled=True)]
    reduce_scatter x1, waiting for transfers between devices: 23.3 us -> 30 us  [local(): lax.psum_scatter(partial_value, 'dom', scatter_dimension=0, tiled=True)]
  transfers between devices with their start and end apart: 12 -> 13, of which waited for: 5 -> 7; matrix products, arithmetic and copies ran while one was open for 12% -> 13% of each run, Pallas kernels for 0% -> 0%
where the time goes in v1:
time: 615 us; the launch traced here: 613 us
  waiting for transfers between devices  370 us (60%)
  other arithmetic  109 us (18%)
  local copies, waits for them, and re-layouts  57.3 us (9%)
  starting transfers between devices  27.1 us (4%)
  blocking collectives  18.7 us (3%)
  matrix products  16.5 us (3%)
  between operations  14.3 us (2%)
    psum x1, waiting for transfers between devices, local(): grad_top = lax.psum(grad_top_partial, ('group', 'dom'))  123 us
    psum x1, waiting for transfers between devices, local(): grad_send = lax.psum(f_weight, ('group', 'dom'))  116 us
    all_gather x1, waiting for transfers between devices, local(): top_total = jnp.sum(lax.all_gather(top_partial, ('group', 'dom')), axis=0)  79.9 us
    reduce_scatter x1, waiting for transfers between devices, local(): lax.psum_scatter(partial_value, 'dom', scatter_dimension=0, tiled=True)  30 us
    scatter-add x2, other arithmetic, edge_forward(): jax.ops.segment_sum(message.astype(jnp.float32), targets, num_segments=ow...  25.4 us
    scatter-add x2, other arithmetic, edge_backward(): jax.ops.segment_sum(jnp.dot(grad_pre, w_recv.T, preferred_element_type=jn...  24.5 us
    scatter-add x2, other arithmetic, edge_backward(): jax.ops.segment_sum(jnp.dot(grad_pre, w_send.T, preferred_element_type=jn...  24.3 us
    reduce_scatter x1, waiting for transfers between devices, local(): lax.psum_scatter(grad_partial, 'dom', scatter_dimension=0, tiled=True)  15.8 us
  transfers between devices with their start and end apart: 13, of which 7 were waited for; matrix products, arithmetic and copies ran while one was open for 13% of the time, Pallas kernels for 0%

profile of v1, /device:TPU:1, one launch (start us, length us, event | category | flops | bytes accessed | tf_op | source)
XLA Modules:
  0.0 612.9 jit_solution(2472457165018205766)
XLA Ops:
  9.6 4.0 collective-permute-start
  17.9 4.7 all-to-all-start
  23.3 12.1 %gather_fusion.3 = bf16[4096,128]{1,0:T(8,128)(2,1)S(1)} fusion(bf16[512,128]{1,0:T(8,128)(2,1)S(1)} %copy-done.1, s32[4096]{0:T(1024)S(1)} %fusion.37), kind=kCustom, calls=%fused_computation.3 | custom fusion | bytes 2113536 | tf_op jit(solution)/shard_map/gather | solution.py:29
  37.3 12.1 %gather_fusion.2 = bf16[4096,128]{1,0:T(8,128)(2,1)S(1)} fusion(bf16[896,128]{1,0:T(8,128)(2,1)S(1)} %pad_maximum_fusion, s32[4096]{0:T(1024)S(1)} %fusion.36), kind=kCustom, calls=%fused_computation.2 | custom fusion | bytes 2113536 | tf_op jit(solution)/shard_map/gather | solution.py:28
  51.5 23.8 %scatter_custom_fusion = f32[512,128]{1,0:T(8,128)} fusion(s32[4096]{0:T(1024)} %param.23, f32[4096,128]{1,0:T(8,128)S(1)} %convolution_add_fusion, f32[]{:T(128)} %constant.20.clone.1, f32[]{:T(128)} %constant.14.clone.1), kind=kCustom, calls=%fused_computation.28 | custom fusion | flops 3670016 | bytes 2360320 | tf_op jit(solution)/shard_map/scatter-add | solution.py:31
  77.2 3.2 scatter_custom_fusion.1
  80.5 3.0 scatter_custom_fusion.4
  85.8 30.0 %reduce-scatter.3.cloned.1.call-done = f32[32,128]{1,0:T(8,128)} async-done(((f32[256,128]{1,0:T(8,128)}), f32[32,128]{1,0:T(8,128)}) %reduce-scatter.3.cloned.1.call-update) | async-done | bytes 16400 | tf_op jit(solution)/shard_map/reduce_scatter | solution.py:116
  117.7 4.5 all-to-all-start.1
  123.0 3.2 all-to-all-done.1
  136.5 15.8 %reduce-scatter.5.cloned.1.call-done = f32[32,128]{1,0:T(8,128)} async-done(((f32[256,128]{1,0:T(8,128)}), f32[32,128]{1,0:T(8,128)}) %reduce-scatter.5.cloned.1.call-update) | async-done | bytes 16400 | tf_op jit(solution)/shard_map/reduce_scatter | solution.py:117
  154.0 79.9 %all-gather.3.cloned.1.call-done = f32[16384,128]{1,0:T(8,128)} async-done(((f32[512,128]{1,0:T(8,128)}), f32[16384,128]{1,0:T(8,128)}) %all-gather.3.cloned.1.call-update) | async-done | bytes 8388624 | tf_op jit(solution)/shard_map/all_gather | solution.py:129
  233.8 4.5 reduce_sum.9
  240.3 122.9 %all-reduce.7.cloned.1.call-done = f32[512,128]{1,0:T(8,128)} async-done(((f32[512,128]{1,0:T(8,128)}), f32[512,128]{1,0:T(8,128)}) %all-reduce.7.cloned.1.call-update) | async-done | bytes 262160 | tf_op jit(solution)/shard_map/psum | solution.py:130
  371.7 5.1 all-to-all-start.2
  379.2 9.6 %all_gather.14 = bf16[256,128]{1,0:T(8,128)(2,1)S(1)} all-gather(bf16[32,128]{1,0:T(8,128)(2,1)S(1)} %add_convert_fusion.2), channel_id=1, replica_groups=mesh['group'=4,'dom'=8] {'dom'}, dimensions={0}, use_global_device_ids=true | all-gather | bytes 73728 | tf_op jit(solution)/shard_map/all_gather | solution.py:136
  395.8 9.2 %all_gather.15 = f32[256,128]{1,0:T(8,128)S(1)} all-gather(f32[32,128]{1,0:T(8,128)S(1)} %slice.78), channel_id=1, replica_groups=mesh['group'=4,'dom'=8] {'dom'}, dimensions={0}, use_global_device_ids=true | all-gather | bytes 147456 | tf_op jit(solution)/shard_map/all_gather | solution.py:153
  407.9 14.1 %gather_fusion.12 = f32[4096,128]{1,0:T(8,128)} fusion(f32[512,128]{1,0:T(8,128)S(1)} %fusion.15, s32[4096]{0:T(1024)S(1)} %fusion.37), kind=kCustom, calls=%fused_computation.12 | custom fusion | bytes 4210688 | tf_op jit(solution)/shard_map/gather | solution.py:43
  422.0 2.4 multiply_convert_fusion
  427.8 22.8 %scatter_custom_fusion.9 = f32[896,128]{1,0:T(8,128)S(1)} fusion(s32[4096]{0:T(1024)} %param.22, f32[4096,128]{1,0:T(8,128)} %fusion.56, f32[]{:T(128)} %constant.14.clone.1), kind=kCustom, calls=%fused_computation.54 | custom fusion | flops 524288 | bytes 459264 | tf_op jit(solution)/shard_map/scatter-add | solution.py:44
  451.2 3.4 all-to-all-start.3
  455.6 22.5 %scatter_fusion.2 = f32[512,128]{1,0:T(8,128)S(1)} fusion(f32[512,128]{1,0:T(8,128)S(1)} %slice_add_fusion, s32[4096]{0:T(1024)S(1)} %copy-done.10, f32[4096,128]{1,0:T(8,128)S(1)} %fusion.57), kind=kCustom, calls=%fused_computation.23 | custom fusion | flops 524288 | bytes 6307840 | tf_op jit(solution)/shard_map/scatter-add | solution.py:50
  478.2 2.7 collective-permute-start.2
  488.7 116.1 %all-reduce.9.cloned.1.call-done = f32[128,128]{1,0:T(8,128)} async-done(((f32[128,128]{1,0:T(8,128)}), f32[128,128]{1,0:T(8,128)}) %all-reduce.9.cloned.1.call-update) | async-done | bytes 65552 | tf_op jit(solution)/shard_map/psum | solution.py:171
  (137 shorter events, 67.1 us)
Async XLA Ops:
  7.2 42.3 %copy-start = (bf16[128,128]{1,0:T(8,128)(2,1)S(1)}, bf16[128,128]{1,0:T(8,128)(2,1)}, u32[]{:S(2)}) copy-start(bf16[128,128]{1,0:T(8,128)(2,1)} %param.29) | copy-start | bytes 98308
  9.6 27.7 %collective-permute-start = (bf16[1,128,128]{2,1,0:T(8,128)(2,1)S(1)}, bf16[1,128,128]{2,1,0:T(8,128)(2,1)S(1)}, u32[]{:S(2)}, u32[]{:S(2)}) collective-permute-start(bf16[1,128,128]{2,1,0:T(8,128)(2,1)S(1)} %get-tuple-element.6), channel_id=1, source_target_pairs={{0,8},{8,16},{16,24},{1,9},{9,17},{17,25},{2,10},{10,18},{18,26},{... | collective-permute-start | bytes 98312 | tf_op jit(solution)/shard_map/ppermute | solution.py:14
  13.6 23.7 %collective-permute-start.1 = (bf16[1,128,128]{2,1,0:T(8,128)(2,1)S(1)}, bf16[1,128,128]{2,1,0:T(8,128)(2,1)S(1)}, u32[]{:S(2)}, u32[]{:S(2)}) collective-permute-start(bf16[1,128,128]{2,1,0:T(8,128)(2,1)S(1)} %get-tuple-element.7), channel_id=1, source_target_pairs={{8,0},{16,8},{24,16},{9,1},{17,9},{25,17},{10,2},{18,10},{26,18},{... | collective-permute-start | bytes 98312 | tf_op jit(solution)/shard_map/ppermute | solution.py:17
  17.9 19.4 %all-to-all-start = ((bf16[8,16,128]{2,1,0:T(8,128)(2,1)}), bf16[8,16,128]{2,1,0:T(8,128)(2,1)S(1)}, u32[]{:S(2)}, u32[]{:S(2)}) async-start(bf16[8,16,128]{2,1,0:T(8,128)(2,1)} %bitcast), calls=%async_computation | async-start | bytes 65536 | tf_op jit(solution)/shard_map/all_to_all | solution.py:105
  22.6 93.1 %reduce-scatter.3.cloned.1.call-start = ((), (), s32[]{:S(2)}) async-start(), calls=%async_computation.6 | async-start | bytes 147456 | tf_op jit(solution)/shard_map/reduce_scatter | solution.py:116
  51.5 29.0 %copy-start.3 = (bf16[512,128]{1,0:T(8,128)(2,1)S(1)}, bf16[512,128]{1,0:T(8,128)(2,1)}, u32[]{:S(2)}) copy-start(bf16[512,128]{1,0:T(8,128)(2,1)} %param.19) | copy-start | bytes 393220
  51.5 75.5 %copy-start.6 = (bf16[128,128]{1,0:T(8,128)(2,1)S(1)}, bf16[128,128]{1,0:T(8,128)(2,1)}, u32[]{:S(2)}) copy-start(bf16[128,128]{1,0:T(8,128)(2,1)} %param.32) | copy-start | bytes 98308
  51.5 75.6 %copy-start.8 = (bf16[128,128]{1,0:T(8,128)(2,1)S(1)}, bf16[128,128]{1,0:T(8,128)(2,1)}, u32[]{:S(2)}) copy-start(bf16[128,128]{1,0:T(8,128)(2,1)} %param.33) | copy-start | bytes 98308
  75.3 53.6 %copy-start.7 = (bf16[128,128]{1,0:T(8,128)(2,1)S(1)}, bf16[128,128]{1,0:T(8,128)(2,1)}, u32[]{:S(2)}) copy-start(bf16[128,128]{1,0:T(8,128)(2,1)} %param.34) | copy-start | bytes 98308
  80.5 71.9 %reduce-scatter.5.cloned.1.call-start = ((), (), s32[]{:S(2)}) async-start(), calls=%async_computation.7 | async-start | bytes 147456 | tf_op jit(solution)/shard_map/reduce_scatter | solution.py:117
  117.7 8.5 %all-to-all-start.1 = ((bf16[8,4,128]{2,1,0:T(4,128)(2,1)}), bf16[8,4,128]{2,1,0:T(4,128)(2,1)S(1)}, u32[]{:S(2)}, u32[]{:S(2)}) async-start(bf16[8,4,128]{2,1,0:T(4,128)(2,1)} %bitcast.7), calls=%async_computation.2 | async-start | bytes 16384 | tf_op jit(solution)/shard_map/all_to_all | solution.py:120
  122.1 111.7 %all-gather.3.cloned.1.call-start = ((), (), s32[]{:S(2)}) async-start(), calls=%async_computation.10 | async-start | bytes 8650752 | tf_op jit(solution)/shard_map/all_gather | solution.py:129
  122.1 116.2 %copy-start.16 = (s32[1024]{0:T(1024)}, s32[1024]{0:T(1024)S(1)}, u32[]{:S(2)}) copy-start(s32[1024]{0:T(1024)S(1)} %pad_clamp_fusion.2) | copy-start | bytes 12292
  129.1 109.3 %copy-start.12 = (f32[32,128]{1,0:T(8,128)}, f32[32,128]{1,0:T(8,128)S(1)}, u32[]{:S(2)}) copy-start(f32[32,128]{1,0:T(8,128)S(1)} %fusion.5) | copy-start | bytes 49156
  130.6 232.6 %all-reduce.7.cloned.1.call-start = ((), (), s32[]{:S(2)}) async-start(), calls=%async_computation.8 | async-start | bytes 524288 | tf_op jit(solution)/shard_map/psum | solution.py:130
  132.9 232.3 %copy-start.17 = (s32[1024]{0:T(1024)}, s32[1024]{0:T(1024)S(1)}, u32[]{:S(2)}) copy-start(s32[1024]{0:T(1024)S(1)} %pad_clamp_fusion.1) | copy-start | bytes 12292
  238.3 128.5 %copy-start.11 = (f32[32,128]{1,0:T(8,128)S(1)}, f32[32,128]{1,0:T(8,128)}, u32[]{:S(2)}) copy-start(f32[32,128]{1,0:T(8,128)} %reduce-scatter.5.cloned.1.call-done) | copy-start | bytes 49156
  371.7 23.2 %all-to-all-start.2 = ((f32[8,4,128]{2,1,0:T(4,128)}), f32[8,4,128]{2,1,0:T(4,128)S(1)}, u32[]{:S(2)}, u32[]{:S(2)}) async-start(f32[8,4,128]{2,1,0:T(4,128)} %bitcast.11), calls=%async_computation.4 | async-start | bytes 32768 | tf_op jit(solution)/shard_map/all_to_all | solution.py:145
  426.6 28.0 %copy-start.2 = (f32[512,128]{1,0:T(8,128)S(1)}, f32[512,128]{1,0:T(8,128)}, u32[]{:S(2)}) copy-start(f32[512,128]{1,0:T(8,128)} %gather_fusion.11) | copy-start | bytes 786436
  426.6 28.9 %copy-start.10 = (s32[4096]{0:T(1024)S(1)}, s32[4096]{0:T(1024)}, u32[]{:S(2)}) copy-start(s32[4096]{0:T(1024)} %param.23) | copy-start | bytes 49156
  451.2 31.0 %all-to-all-start.3 = ((f32[8,16,128]{2,1,0:T(8,128)}), f32[8,16,128]{2,1,0:T(8,128)S(1)}, u32[]{:S(2)}, u32[]{:S(2)}) async-start(f32[8,16,128]{2,1,0:T(8,128)} %bitcast.14), calls=%async_computation.5 | async-start | bytes 131072 | tf_op jit(solution)/shard_map/all_to_all | solution.py:159
  454.6 150.3 %all-reduce.9.cloned.1.call-start = ((), (), s32[]{:S(2)}) async-start(), calls=%async_computation.9 | async-start | bytes 131072 | tf_op jit(solution)/shard_map/psum | solution.py:171
  478.2 5.6 collective-permute-start.2
  480.9 5.0 collective-permute-start.3
  (10 other events, 152.8 us)
Sparse Core Ops, SparseCore 0:
  80.6 35.1 reduce-scatter.2
  118.7 33.5 reduce-scatter.4
  155.8 77.9 all-gather.2
  239.2 123.9 all-reduce.6
  482.3 122.5 all-reduce.8
